TPU v7x, 32 devices: a whole 2x2x4 slice. The times are simulated.
32 devices in a mesh: section: 4 (over z), fsdp: 4 (over y, core), tp: 2 (over x).
Axes of the slice: x: 2, y: 2, z: 4, core: 2. Of those that a mesh axis runs over, the one named last changes fastest.
Arguments:
- stash: bfloat16 [4, 4, 512, 2304], P('section', None, 'fsdp'), may hold values from -6 to 6
- grad_now: bfloat16 [4, 512, 2304], P('section', 'fsdp'), may hold values from -6 to 6
- grad_top: bfloat16 [2, 512, 2304], P(None, 'fsdp'), may hold values from -6 to 6
- order: int32 [4, 4], P('section'), may hold values from 0 to 3, each once within a row
- gain: float32 [4, 2304], P('section'), may hold values from 0.5 to 1.5
- weight: bfloat16 [4, 2304, 2048], P('section', 'fsdp', 'tp'), may hold values from -0.125 to 0.125
Outputs:
- grad_held: bfloat16 [4, 512, 2304], P('section', 'fsdp')
- weight_grad: float32 [4, 2304, 2048], P('section', 'fsdp', 'tp')
Inputs may be any that keep to these rules, and one draw needn't show every extreme that they name: Each row of order names every kept micro-batch once.
All inputs are finite; a program needn't handle non-finite values.
Results may differ from a plain program's by a relative error of at most 0.013.
Values may be sent and summed in bfloat16 or wider, within the bound.
A program may use at most 64 MiB of HBM per device.

v0:
```python
import functools

import jax
import jax.numpy as jnp
from jax import lax
from jax.experimental import pallas as pl
from jax.experimental.pallas import tpu as pltpu
from jax.sharding import PartitionSpec as P

norm_eps = 1e-06
MESH = pl.DeviceIdType.MESH
f32 = jnp.float32
bf16 = jnp.bfloat16
LAG = 2


def gelu_parts(u):
    k = 0.7978845608028654
    c = 0.044715
    u2 = u * u
    t = jnp.tanh(k * u * (1.0 + c * u2))
    half = 0.5 * (1.0 + t)
    act = u * half
    slope = half + 0.5 * u * (1.0 - t * t) * (k * (1.0 + 3.0 * c * u2))
    return act, slope


def pick(extent, options):
    for o in options:
        if extent % o == 0:
            return o
    return extent


def kernel(
    S, FS, TP, T, order_ref, gain_ref, stash_ref, gnow_ref, gtop_ref, w_ref,
    held_ref, wg_ref,
    wfull, stash, act, xt, inv, dyn, lt, lta, rhs, prod, slope, own_e, peer_e, dxs, acc,
    lsem, topsem, ownsem, heldsem, w_s, w_r, l_s, l_r, r_s, r_r, e_s, e_r, z_s, z_r, x_s, x_r,
):
    s = lax.axis_index("section")
    f = lax.axis_index("fsdp")
    p = lax.axis_index("tp")
    NC = FS // 2
    yc = f // 2
    core = f % 2
    sib = 2 * yc + (1 - core)
    n, D = act.shape[0] // (T + 1), act.shape[1]
    wl, N = w_ref.shape[1], w_ref.shape[2]
    WCH = w_s.shape[1]
    wq = wl // TP
    SPLIT = tuple(2 * t for t in range(T)) + (1,)
    wc = wl // WCH
    CW = D // e_s.shape[-1]
    CH = D // CW
    nw = pick(N, (256, 128))

    loads = [
        pltpu.make_async_copy(w_ref.at[0], wfull.at[pl.ds(f * wl, wl), :], lsem.at[0]),
        pltpu.make_async_copy(stash_ref.at[0], stash, lsem.at[1]),
        pltpu.make_async_copy(gnow_ref.at[0], act.at[pl.ds(T * n, n), :], lsem.at[2]),
    ]
    for c in loads:
        c.start()

    bar = pltpu.get_barrier_semaphore()
    for r in range(1, FS):
        pl.semaphore_signal(bar, inc=1, device_id={"fsdp": (f + r) % FS}, device_id_type=MESH)
    for r in range(1, TP):
        pl.semaphore_signal(bar, inc=1, device_id={"tp": (p + r) % TP}, device_id_type=MESH)

    @pl.when(s > 0)
    def _():
        pl.semaphore_signal(bar, inc=1, device_id={"section": s - 1}, device_id_type=MESH)

    @pl.when(s < S - 1)
    def _():
        pl.semaphore_signal(bar, inc=1, device_id={"section": s + 1}, device_id_type=MESH)

    pl.semaphore_wait(bar, FS - 1 + TP - 1 + jnp.minimum(s, 1) + jnp.minimum(S - 1 - s, 1))

    def rcopy(src, dst, ss, rs, dev):
        return pltpu.make_async_remote_copy(
            src_ref=src, dst_ref=dst, send_sem=ss, recv_sem=rs, device_id=dev, device_id_type=MESH
        )

    def w_copy(k, j):
        if k < NC:
            rows = pl.ds(f * wl + j * wc, wc)
            src = w_ref.at[0, pl.ds(j * wc, wc), :]
            to = sib if k == 0 else 2 * ((yc + k) % NC) + core
        else:
            o = k - NC + 1
            rows = pl.ds((2 * ((yc - o + NC) % NC) + core) * wl + j * wc, wc)
            src = wfull.at[rows, :]
            to = sib
        return rcopy(src, wfull.at[rows, :], w_s.at[k, j], w_r.at[k, j], {"fsdp": to})

    for k in list(range(1, NC)) + [0]:
        for j in range(WCH):
            w_copy(k, j).start()

    def is_split(part):
        return part in SPLIT and TP > 1

    def l_copy(part, k):
        cols = pl.ds(pl.multiple_of(f * n, n), n)
        if k == 0:
            to = sib
        else:
            o, cc = (k + 1) // 2, (k - 1) % 2
            to = 2 * ((yc + o) % NC) + (core + cc) % 2
        if k > 0 and is_split(part):
            src = lt.at[part, pl.ds(to * wl + p * wq, wq), :]
            dst = lta.at[part, pl.ds(p * wq, wq), cols]
        else:
            src = lt.at[part, pl.ds(to * wl, wl), :]
            dst = lta.at[part, :, cols]
        return rcopy(src, dst, l_s.at[part, k], l_r.at[part, k], {"fsdp": to})

    def x_copy(part, k, q):
        o, cc = (k + 1) // 2, (k - 1) % 2
        src_f = 2 * ((yc - o + NC) % NC) + (core + cc) % 2
        blk = lta.at[part, pl.ds(p * wq, wq), pl.ds(pl.multiple_of(src_f * n, n), n)]
        return rcopy(blk, blk, x_s.at[part, k - 1, q - 1], x_r.at[part, k - 1, q - 1], {"tp": (p + q) % TP})

    passed = set()

    def l_pass(part):
        if part in passed or not is_split(part):
            return
        passed.add(part)
        for k in range(1, FS - 1):
            l_copy(part, k).wait_recv()
            for q in range(1, TP):
                x_copy(part, k, q).start()

    def l_own(part):
        return pltpu.make_async_copy(
            lt.at[part, pl.ds(f * wl, wl), :], lta.at[part, :, pl.ds(pl.multiple_of(f * n, n), n)],
            ownsem.at[part],
        )

    def l_send(part):
        for k in list(range(1, FS - 1)) + [0]:
            l_copy(part, k).start()
        l_own(part).start()

    def r_copy(part, k):
        if k < NC:
            at = f
            to = sib if k == 0 else 2 * ((yc + k) % NC) + core
        else:
            o = k - NC + 1
            at = 2 * ((yc - o + NC) % NC) + core
            to = sib
        blk = rhs.at[part, pl.ds(pl.multiple_of(at * n, n), n), :]
        return rcopy(blk, blk, r_s.at[part, k], r_r.at[part, k], {"fsdp": to})

    def r_send(part):
        for k in list(range(1, NC)) + [0]:
            r_copy(part, k).start()

    tw = pick(D, (256, 128))

    def transpose_rows(part, ref, first):
        @pl.loop(0, D // tw)
        def _(i):
            cols = pl.ds(pl.multiple_of(i * tw, tw), tw)
            lt[part, cols, :] = ref[pl.ds(first, n), cols].astype(f32).T.astype(bf16)

    loads[1].wait()
    rb = pick(n, (32, 16))
    for t in range(T):
        slot = order_ref[0, t]

        @pl.loop(0, n // rb)
        def _(i):
            rows = pl.ds(pl.multiple_of(i * rb, rb), rb)
            raw = stash[slot, rows, :]
            v = raw.astype(f32)
            iv = lax.rsqrt(jnp.mean(v * v, axis=-1, keepdims=True) + norm_eps)
            xt[t, rows, :] = raw
            inv[t, rows, :] = jnp.broadcast_to(iv, (rb, 128))
            act[pl.ds(pl.multiple_of(t * n + i * rb, rb), rb), :] = ((v * iv) * gain_ref[0:1, :]).astype(bf16)

        transpose_rows(2 * t, act, t * n)
        if t == 0:
            l_send(0)
            loads[2].wait()
            transpose_rows(1, act, T * n)
            l_send(1)
        else:
            l_send(2 * t)

    @pl.when(s == S - 1)
    def _():
        for t in range(T):
            pltpu.make_async_copy(gtop_ref.at[t], dyn.at[t], topsem.at[t]).start()

    half = 2 * wl

    def part_product(chip, first):
        ks = pl.ds(pl.multiple_of(chip * half, half), half)

        @pl.loop(0, N // nw)
        def _(i):
            cols = pl.ds(pl.multiple_of(i * nw, nw), nw)
            d = jnp.dot(act[:, ks], wfull[ks, cols], preferred_element_type=f32)
            if first:
                prod[:, cols] = d
            else:
                prod[:, cols] += d

    loads[0].wait()
    for j in range(WCH):
        w_copy(0, j).wait_recv()
    part_product(yc, True)
    for o in range(1, NC):
        for j in range(WCH):
            w_copy(o, j).wait_recv()
            w_copy(NC - 1 + o, j).start()
        for j in range(WCH):
            w_copy(NC - 1 + o, j).wait_recv()
        part_product((yc - o + NC) % NC, False)

    mine = pl.multiple_of(f * n, n)

    def gelu_rows(t, with_grad):
        @pl.loop(0, n // rb)
        def _(i):
            rows = pl.ds(pl.multiple_of(t * n + i * rb, rb), rb)
            here = pl.ds(pl.multiple_of(mine + i * rb, rb), rb)
            a, sl = gelu_parts(prod[rows, :])
            rhs[2 * t + 1, here, :] = a.astype(bf16)
            if with_grad:
                g = prod[pl.ds(pl.multiple_of(T * n + i * rb, rb), rb), :]
                rhs[2 * t, here, :] = (sl * g).astype(bf16)
            else:
                slope[t, pl.ds(pl.multiple_of(i * rb, rb), rb), :] = sl

    def e_copy(t, r, c):
        cols = pl.ds(pl.multiple_of(c * CW, CW), CW)
        return rcopy(
            own_e.at[t, :, cols], peer_e.at[t, r - 1, :, cols],
            e_s.at[t, r - 1, c], e_r.at[t, r - 1, c], {"tp": (p + r) % TP},
        )

    def z_copy(t, c):
        cols = pl.ds(pl.multiple_of(c * CW, CW), CW)
        to = jnp.maximum(s - 1, 0)
        return rcopy(
            dxs.at[t, :, cols], dyn.at[t, :, cols], z_s.at[t, c], z_r.at[t, c], {"section": to}
        )

    def spread(t):
        du = rhs[2 * t, pl.ds(mine, n), :]
        u = prod[pl.ds(t * n, n), :]
        m = jnp.sum(du.astype(f32) * u, axis=-1, keepdims=True) / D
        iv = inv[t, :, 0:1]
        q_scale = iv * iv * m

        @pl.loop(0, CH)
        def _(c):
            cols = pl.ds(pl.multiple_of(c * CW, CW), CW)
            dh = lax.dot_general(
                rhs[2 * t, pl.ds(mine, n), :], wfull[cols, :], (((1,), (1,)), ((), ())),
                preferred_element_type=f32,
            )
            e = iv * (gain_ref[0:1, cols] * dh) - xt[t, :, cols].astype(f32) * q_scale
            own_e[t, :, cols] = e.astype(bf16)
            for r in range(1, TP):
                e_copy(t, r, c).start()

    def combine(t, c):
        cols = pl.ds(pl.multiple_of(c * CW, CW), CW)
        for r in range(1, TP):
            e_copy(t, r, c).wait_recv()
        total = own_e[t, :, cols].astype(f32)
        for r in range(1, TP):
            total = total + peer_e[t, r - 1, :, cols].astype(f32)
        dy = act[pl.ds(T * n, n), cols] if t == 0 else dyn[t - 1, :, cols]
        dxs[t, :, cols] = (dy.astype(f32) + total).astype(bf16)
        z_copy(t, c).start()

    parts = []
    for t in range(T):
        parts += [2 * t, 2 * t + 1] if t == 0 else [2 * t + 1, 2 * t]

    def own_rows(at):
        part = parts[at]
        l_pass(part)
        l_own(part).wait()
        l_copy(part, 0).wait_recv()
        for k in range(1, FS - 1):
            if is_split(part):
                for q in range(1, TP):
                    x_copy(part, k, q).wait_recv()
            else:
                l_copy(part, k).wait_recv()
        for o in range(1, NC):
            r_copy(part, o).wait_recv()
            r_copy(part, NC - 1 + o).start()
        r_copy(part, 0).wait_recv()
        for o in range(1, NC):
            r_copy(part, NC - 1 + o).wait_recv()
        final = at == len(parts) - 1

        @pl.loop(0, N // nw)
        def _(i):
            cols = pl.ds(pl.multiple_of(i * nw, nw), nw)
            d = jnp.dot(lta[part], rhs[part, :, cols], preferred_element_type=f32)
            if at > 0:
                d = acc[:, cols] + d
            if final:
                wg_ref[0, :, cols] = d.astype(bf16)
            else:
                acc[:, cols] = d

    for t in range(T):
        if t == 0:
            gelu_rows(0, True)
        r_ids = [0, 1] if t == 0 else [2 * t]

        @pl.when(s > 0)
        def _():
            spread(t)

        for part in r_ids:
            r_send(part)
        if t == 0:
            for later in range(1, T):
                gelu_rows(later, False)
                r_send(2 * later + 1)

        if t < T - 1:
            @pl.when(s == S - 1)
            def _():
                pltpu.make_async_copy(gtop_ref.at[t], dyn.at[t], topsem.at[t]).wait()

            gr = pl.ds(T * n, n)

            @pl.loop(0, CH + LAG)
            def _(i):
                @pl.when((i < CH) & (s > 0))
                def _():
                    combine(t, i)

                if t == 0:
                    @pl.when(i == CH // 2)
                    def _():
                        l_pass(0)

                    @pl.when(i == CH - 1)
                    def _():
                        l_pass(1)

                @pl.when(i >= LAG)
                def _():
                    c = i - LAG

                    @pl.when(s < S - 1)
                    def _():
                        z_copy(t, c).wait_recv()

                    cols = pl.ds(pl.multiple_of(c * CW, CW), CW)
                    d = dyn[t, :, cols]
                    lt[2 * t + 3, cols, :] = d.astype(f32).T.astype(bf16)
                    g = jnp.dot(d, wfull[cols, :], preferred_element_type=f32)

                    @pl.when(c == 0)
                    def _():
                        prod[gr, :] = g

                    @pl.when(c > 0)
                    def _():
                        prod[gr, :] += g

            l_send(2 * t + 3)

            @pl.loop(0, n // rb)
            def _(i):
                rows = pl.ds(pl.multiple_of(i * rb, rb), rb)
                g = prod[pl.ds(pl.multiple_of(T * n + i * rb, rb), rb), :]
                here = pl.ds(pl.multiple_of(mine + i * rb, rb), rb)
                rhs[2 * t + 2, here, :] = (slope[t + 1, rows, :] * g).astype(bf16)
        else:
            for at in range(max(2 * T - 2, 0)):
                own_rows(at)
            for part in SPLIT:
                l_pass(part)

            @pl.when(s > 0)
            def _():
                @pl.loop(0, CH)
                def _(c):
                    combine(t, c)

    for at in range(max(2 * T - 2, 0), 2 * T):
        own_rows(at)

    t = T - 1

    @pl.when(s == S - 1)
    def _():
        pltpu.make_async_copy(gtop_ref.at[t], dyn.at[t], topsem.at[t]).wait()

    @pl.when(s < S - 1)
    def _():
        @pl.loop(0, CH)
        def _(c):
            z_copy(t, c).wait_recv()

    out = pltpu.make_async_copy(dyn.at[t], held_ref.at[0], heldsem.at[0])
    out.start()

    for j in range(WCH):
        for k in range(2 * NC - 1):
            w_copy(k, j).wait_send()
    for part in range(2 * T):
        for k in range(FS - 1):
            l_copy(part, k).wait_send()
        if is_split(part):
            for k in range(1, FS - 1):
                for q in range(1, TP):
                    x_copy(part, k, q).wait_send()
        for k in range(2 * NC - 1):
            r_copy(part, k).wait_send()

    @pl.when(s > 0)
    def _():
        for t in range(T):
            @pl.loop(0, CH)
            def _(c):
                for r in range(1, TP):
                    e_copy(t, r, c).wait_send()
                z_copy(t, c).wait_send()

    out.wait()


def solution(mesh):
    S, FS, TP = mesh.shape["section"], mesh.shape["fsdp"], mesh.shape["tp"]

    def per_device(stash, grad_now, grad_top, order, gain, weight):
        MB, n, D = stash.shape[1:]
        T = grad_top.shape[0]
        wl, N = weight.shape[1:]
        NC = FS // 2
        CH = D // pick(D, (384, 256, 128))
        WCH = 4 if wl % 64 == 0 else 1
        K = 2 * NC - 1
        DMA = pltpu.SemaphoreType.DMA
        V = pltpu.VMEM
        any_ = pl.BlockSpec(memory_space=pl.ANY)
        peers = max(TP - 1, 1)
        held, wg = pl.pallas_call(
            functools.partial(kernel, S, FS, TP, T),
            out_shape=(
                jax.ShapeDtypeStruct((1, n, D), bf16),
                jax.ShapeDtypeStruct((1, wl, N), bf16),
            ),
            in_specs=[
                pl.BlockSpec(memory_space=pltpu.SMEM),
                pl.BlockSpec(memory_space=pltpu.VMEM),
                any_, any_, any_, any_,
            ],
            out_specs=(any_, pl.BlockSpec(memory_space=pltpu.VMEM)),
            scratch_shapes=[
                V((FS * wl, N), bf16),
                V((MB, n, D), bf16),
                V(((T + 1) * n, D), bf16),
                V((T, n, D), bf16),
                V((T, n, 128), f32),
                V((T, n, D), bf16),
                V((2 * T, D, n), bf16),
                V((2 * T, wl, FS * n), bf16),
                V((2 * T, FS * n, N), bf16),
                V(((T + 1) * n, N), f32),
                V((T, n, N), f32),
                V((T, n, D), bf16),
                V((T, peers, n, D), bf16),
                V((T, n, D), bf16),
                V((wl, N), f32),
                DMA((3,)), DMA((T,)), DMA((2 * T,)), DMA((1,)),
                DMA((K, WCH)), DMA((K, WCH)),
                DMA((2 * T, FS - 1)), DMA((2 * T, FS - 1)),
                DMA((2 * T, K)), DMA((2 * T, K)),
                DMA((T, peers, CH)), DMA((T, peers, CH)),
                DMA((T, CH)), DMA((T, CH)),
                DMA((2 * T, max(FS - 2, 1), peers)), DMA((2 * T, max(FS - 2, 1), peers)),
            ],
            compiler_params=pltpu.CompilerParams(
                collective_id=0, has_side_effects=True, vmem_limit_bytes=60 * 1024 * 1024
            ),
        )(order, gain, stash, grad_now, grad_top, weight)
        return held, wg.astype(f32)

    return jax.shard_map(
        per_device,
        mesh=mesh,
        in_specs=(
            P("section", None, "fsdp", None),
            P("section", "fsdp", None),
            P(None, "fsdp", None),
            P("section", None),
            P("section", None),
            P("section", "fsdp", "tp"),
        ),
        out_specs=(P("section", "fsdp", None), P("section", "fsdp", "tp")),
        check_vma=False,
    )
```

profile of v0, /device:TPU:0, one launch (start us, length us, event | category | flops | bytes accessed | tf_op | source)
XLA Modules:
  0.0 85.6 jit_solution(13358794173078146086)
XLA Ops:
  0.6 81.1 %shard_map.77 = (bf16[1,128,2304]{2,1,0:T(8,128)(2,1)}, bf16[1,576,1024]{2,1,0:T(8,128)(2,1)}) custom-call(s32[1,4]{1,0:T(1,128)} %order_ref.1, f32[1,2304]{1,0:T(1,128)} %gain_ref.1, bf16[1,4,128,2304]{3,2,1,0:T(8,128)(2,1)} %stash_ref.1, bf16[1,128,2304]{2,1,0:T(8,128)(2,1)} %gnow_ref.1, bf16[2,128,2304]{2,1,0:T(8,128)(2,1)} %gtop_ref.1, ...), custom_call_target="tpu_custom_call" | custom-call | tf_op jit(solution)/shard_map/pallas_call | solution.py:457
  81.7 0.0 copy-start
  81.7 3.0 %convert_element_type.3 = f32[1,576,1024]{2,1,0:T(8,128)} convert(bf16[1,576,1024]{2,1,0:T(8,128)(2,1)} %get-tuple-element.5) | non-fusion elementwise | flops 589824 | bytes 3538944 | tf_op jit(solution)/shard_map/convert_element_type | solution.py:497
  84.8 0.0 copy-done
  84.8 0.8 copy.9
Async XLA Ops:
  81.7 3.0 %copy-start = (bf16[1,128,2304]{2,1,0:T(8,128)(2,1)S(1)}, bf16[1,128,2304]{2,1,0:T(8,128)(2,1)}, u32[]{:S(2)}) copy-start(bf16[1,128,2304]{2,1,0:T(8,128)(2,1)} %get-tuple-element.8) | copy-start | bytes 1769476
where the time goes:
time: 85.8 us; the launch traced here: 85.6 us
  Pallas kernels  81.1 us (95%)
  other arithmetic  3.02 us (4%)
    pallas_call x1, Pallas kernels, per_device(): pl.pallas_call(functools.partial(kernel, S, FS, TP, T), out_shape=(jax.Sh...  81.1 us
    convert_element_type x1, other arithmetic, per_device(): return (held, wg.astype(f32))  3.02 us

commit v1 on v0

--- a/solution.py
+++ b/solution.py
@@ -1,4 +1,5 @@
 import functools
+import math
 
 import jax
 import jax.numpy as jnp
@@ -11,7 +12,7 @@
 MESH = pl.DeviceIdType.MESH
 f32 = jnp.float32
 bf16 = jnp.bfloat16
-LAG = 2
+LAG = 3
 
 
 def gelu_parts(u):
@@ -32,11 +33,23 @@
     return extent
 
 
+def w_cuts(wl):
+    if wl % 64 or wl <= 128:
+        return (0, wl)
+    deep = wl // 128 * 128
+    cuts = list(range(0, deep, 256)) + [deep]
+    return tuple(cuts) if deep == wl else tuple(cuts) + (wl,)
+
+
+def row_step(wl):
+    return math.gcd(wl, 64)
+
+
 def kernel(
     S, FS, TP, T, order_ref, gain_ref, stash_ref, gnow_ref, gtop_ref, w_ref,
-    held_ref, wg_ref,
-    wfull, stash, act, xt, inv, dyn, lt, lta, rhs, prod, slope, own_e, peer_e, dxs, acc,
-    lsem, topsem, ownsem, heldsem, w_s, w_r, l_s, l_r, r_s, r_r, e_s, e_r, z_s, z_r, x_s, x_r,
+    held_ref, acc, lta, rhs,
+    wfull, stash, act, xt, inv, dyn, lt, prod, slope, own_e, peer_e, dxs, zin, peer_f,
+    lsem, topsem, ownsem, w_s, w_r, l_s, l_r, r_s, r_r, e_s, e_r, z_s, z_r, x_s, x_r, f_s, f_r,
 ):
     s = lax.axis_index("section")
     f = lax.axis_index("fsdp")
@@ -47,13 +60,15 @@
     sib = 2 * yc + (1 - core)
     n, D = act.shape[0] // (T + 1), act.shape[1]
     wl, N = w_ref.shape[1], w_ref.shape[2]
-    WCH = w_s.shape[1]
+    cuts = w_cuts(wl)
+    WCH = len(cuts) - 1
     wq = wl // TP
-    SPLIT = tuple(2 * t for t in range(T)) + (1,)
-    wc = wl // WCH
     CW = D // e_s.shape[-1]
     CH = D // CW
     nw = pick(N, (256, 128))
+    tiles = N // nw
+    here = CH * s // S
+    there = CH * (s + 1) // S
 
     loads = [
         pltpu.make_async_copy(w_ref.at[0], wfull.at[pl.ds(f * wl, wl), :], lsem.at[0]),
@@ -85,13 +100,15 @@
         )
 
     def w_copy(k, j):
+        lo, hi = cuts[j], cuts[j + 1]
+        at = pl.multiple_of(lo + core * (wl - hi - lo), row_step(wl))
         if k < NC:
-            rows = pl.ds(f * wl + j * wc, wc)
-            src = w_ref.at[0, pl.ds(j * wc, wc), :]
+            rows = pl.ds(pl.multiple_of(f * wl + at, row_step(wl)), hi - lo)
+            src = w_ref.at[0, pl.ds(at, hi - lo), :]
             to = sib if k == 0 else 2 * ((yc + k) % NC) + core
         else:
             o = k - NC + 1
-            rows = pl.ds((2 * ((yc - o + NC) % NC) + core) * wl + j * wc, wc)
+            rows = pl.ds(pl.multiple_of((2 * ((yc - o + NC) % NC) + core) * wl + at, row_step(wl)), hi - lo)
             src = wfull.at[rows, :]
             to = sib
         return rcopy(src, wfull.at[rows, :], w_s.at[k, j], w_r.at[k, j], {"fsdp": to})
@@ -101,7 +118,7 @@
             w_copy(k, j).start()
 
     def is_split(part):
-        return part in SPLIT and TP > 1
+        return TP > 1
 
     def l_copy(part, k):
         cols = pl.ds(pl.multiple_of(f * n, n), n)
@@ -196,17 +213,19 @@
     @pl.when(s == S - 1)
     def _():
         for t in range(T):
-            pltpu.make_async_copy(gtop_ref.at[t], dyn.at[t], topsem.at[t]).start()
+            pltpu.make_async_copy(gtop_ref.at[t], zin.at[t], topsem.at[t]).start()
 
     half = 2 * wl
 
-    def part_product(chip, first):
-        ks = pl.ds(pl.multiple_of(chip * half, half), half)
-
-        @pl.loop(0, N // nw)
+    def part_product(chip, spans, first):
+        @pl.loop(0, tiles)
         def _(i):
             cols = pl.ds(pl.multiple_of(i * nw, nw), nw)
-            d = jnp.dot(act[:, ks], wfull[ks, cols], preferred_element_type=f32)
+            d = None
+            for lo, hi in spans:
+                ks = pl.ds(pl.multiple_of(chip * half + lo, math.gcd(half, lo)), hi - lo)
+                one = jnp.dot(act[:, ks], wfull[ks, cols], preferred_element_type=f32)
+                d = one if d is None else d + one
             if first:
                 prod[:, cols] = d
             else:
@@ -215,14 +234,15 @@
     loads[0].wait()
     for j in range(WCH):
         w_copy(0, j).wait_recv()
-    part_product(yc, True)
+    part_product(yc, [(0, half)], True)
     for o in range(1, NC):
         for j in range(WCH):
             w_copy(o, j).wait_recv()
             w_copy(NC - 1 + o, j).start()
-        for j in range(WCH):
             w_copy(NC - 1 + o, j).wait_recv()
-        part_product((yc - o + NC) % NC, False)
+            lo, hi = cuts[j], cuts[j + 1]
+            spans = [(lo, half - lo)] if hi == wl else [(lo, hi), (half - hi, half - lo)]
+            part_product((yc - o + NC) % NC, spans, False)
 
     mine = pl.multiple_of(f * n, n)
 
@@ -230,12 +250,12 @@
         @pl.loop(0, n // rb)
         def _(i):
             rows = pl.ds(pl.multiple_of(t * n + i * rb, rb), rb)
-            here = pl.ds(pl.multiple_of(mine + i * rb, rb), rb)
+            home = pl.ds(pl.multiple_of(mine + i * rb, rb), rb)
             a, sl = gelu_parts(prod[rows, :])
-            rhs[2 * t + 1, here, :] = a.astype(bf16)
+            rhs[2 * t + 1, home, :] = a.astype(bf16)
             if with_grad:
                 g = prod[pl.ds(pl.multiple_of(T * n + i * rb, rb), rb), :]
-                rhs[2 * t, here, :] = (sl * g).astype(bf16)
+                rhs[2 * t, home, :] = (sl * g).astype(bf16)
             else:
                 slope[t, pl.ds(pl.multiple_of(i * rb, rb), rb), :] = sl
 
@@ -246,12 +266,22 @@
             e_s.at[t, r - 1, c], e_r.at[t, r - 1, c], {"tp": (p + r) % TP},
         )
 
-    def z_copy(t, c):
+    def f_copy(t, r, c):
+        cols = pl.ds(pl.multiple_of(c * CW, CW), CW)
+        return rcopy(
+            zin.at[t, :, cols], peer_f.at[t, r - 1, :, cols],
+            f_s.at[t, r - 1, c], f_r.at[t, r - 1, c], {"tp": (p + r) % TP},
+        )
+
+    def z_copy(t, c, src):
         cols = pl.ds(pl.multiple_of(c * CW, CW), CW)
         to = jnp.maximum(s - 1, 0)
         return rcopy(
-            dxs.at[t, :, cols], dyn.at[t, :, cols], z_s.at[t, c], z_r.at[t, c], {"section": to}
+            src.at[t, :, cols], zin.at[t, :, cols], z_s.at[t, c], z_r.at[t, c], {"section": to}
         )
+
+    def held_dy(t, cols):
+        return (act[pl.ds(T * n, n), cols] if t == 0 else dyn[t - 1, :, cols]).astype(f32)
 
     def spread(t):
         du = rhs[2 * t, pl.ds(mine, n), :]
@@ -261,16 +291,24 @@
         q_scale = iv * iv * m
 
         @pl.loop(0, CH)
-        def _(c):
+        def _(i):
+            c = CH - 1 - i
             cols = pl.ds(pl.multiple_of(c * CW, CW), CW)
             dh = lax.dot_general(
                 rhs[2 * t, pl.ds(mine, n), :], wfull[cols, :], (((1,), (1,)), ((), ())),
                 preferred_element_type=f32,
             )
             e = iv * (gain_ref[0:1, cols] * dh) - xt[t, :, cols].astype(f32) * q_scale
-            own_e[t, :, cols] = e.astype(bf16)
-            for r in range(1, TP):
-                e_copy(t, r, c).start()
+            own_e[t, :, cols] = jnp.where((c >= here) & (p == 0), e + held_dy(t, cols), e).astype(bf16)
+
+            @pl.when(c >= here)
+            def _():
+                z_copy(t, c, own_e).start()
+
+            @pl.when(c < here)
+            def _():
+                for r in range(1, TP):
+                    e_copy(t, r, c).start()
 
     def combine(t, c):
         cols = pl.ds(pl.multiple_of(c * CW, CW), CW)
@@ -279,17 +317,79 @@
         total = own_e[t, :, cols].astype(f32)
         for r in range(1, TP):
             total = total + peer_e[t, r - 1, :, cols].astype(f32)
-        dy = act[pl.ds(T * n, n), cols] if t == 0 else dyn[t - 1, :, cols]
-        dxs[t, :, cols] = (dy.astype(f32) + total).astype(bf16)
-        z_copy(t, c).start()
+        dxs[t, :, cols] = (held_dy(t, cols) + total).astype(bf16)
+        z_copy(t, c, dxs).start()
+
+    def forward(t, c):
+        z_copy(t, c, dxs).wait_recv()
+        for r in range(1, TP):
+            f_copy(t, r, c).start()
+
+    def put(t, cols, value):
+        if t == T - 1:
+            held_ref[0, :, cols] = value
+        else:
+            dyn[t, :, cols] = value
+
+    def arrive(t, c):
+        cols = pl.ds(pl.multiple_of(c * CW, CW), CW)
+
+        @pl.when((c < there) & (s < S - 1))
+        def _():
+            z_copy(t, c, dxs).wait_recv()
+
+        @pl.when(c < there)
+        def _():
+            put(t, cols, zin[t, :, cols])
+
+        @pl.when(c >= there)
+        def _():
+            total = zin[t, :, cols].astype(f32)
+            for r in range(1, TP):
+                f_copy(t, r, c).wait_recv()
+                total = total + peer_f[t, r - 1, :, cols].astype(f32)
+            put(t, cols, total.astype(bf16))
+
+        return cols
+
+    def relay_loop(t, consume, service):
+        @pl.loop(0, CH + LAG)
+        def _(i):
+            @pl.when(i < CH - there)
+            def _():
+                forward(t, CH - 1 - i)
+
+            @pl.when(i < here)
+            def _():
+                combine(t, here - 1 - i)
+
+            service(i)
+
+            @pl.when(i >= LAG)
+            def _():
+                j = i - LAG
+                consume(j, CH - 1 - j)
+
+    def at_step(i, step, fn):
+        @pl.when(i == step)
+        def _():
+            fn()
+
+    relayed = set()
+
+    def r_relay(part):
+        if part in relayed:
+            return
+        relayed.add(part)
+        for o in range(1, NC):
+            r_copy(part, o).wait_recv()
+            r_copy(part, NC - 1 + o).start()
 
     parts = []
     for t in range(T):
         parts += [2 * t, 2 * t + 1] if t == 0 else [2 * t + 1, 2 * t]
 
-    def own_rows(at):
-        part = parts[at]
-        l_pass(part)
+    def own_wait(part):
         l_own(part).wait()
         l_copy(part, 0).wait_recv()
         for k in range(1, FS - 1):
@@ -298,121 +398,115 @@
                     x_copy(part, k, q).wait_recv()
             else:
                 l_copy(part, k).wait_recv()
-        for o in range(1, NC):
-            r_copy(part, o).wait_recv()
-            r_copy(part, NC - 1 + o).start()
         r_copy(part, 0).wait_recv()
         for o in range(1, NC):
             r_copy(part, NC - 1 + o).wait_recv()
-        final = at == len(parts) - 1
-
-        @pl.loop(0, N // nw)
-        def _(i):
-            cols = pl.ds(pl.multiple_of(i * nw, nw), nw)
-            d = jnp.dot(lta[part], rhs[part, :, cols], preferred_element_type=f32)
-            if at > 0:
-                d = acc[:, cols] + d
-            if final:
-                wg_ref[0, :, cols] = d.astype(bf16)
-            else:
-                acc[:, cols] = d
+
+    def own_tile(at, i):
+        part = parts[at]
+        cols = pl.ds(pl.multiple_of(i * nw, nw), nw)
+        d = jnp.dot(lta[part], rhs[part, :, cols], preferred_element_type=f32)
+        if at > 0:
+            d = acc[:, cols] + d
+        acc[:, cols] = d
 
     for t in range(T):
+        last = t == T - 1
         if t == 0:
             gelu_rows(0, True)
-        r_ids = [0, 1] if t == 0 else [2 * t]
+            r_send(0)
+            r_send(1)
+        else:
+            r_send(2 * t)
 
         @pl.when(s > 0)
         def _():
             spread(t)
 
-        for part in r_ids:
-            r_send(part)
         if t == 0:
             for later in range(1, T):
                 gelu_rows(later, False)
                 r_send(2 * later + 1)
 
-        if t < T - 1:
-            @pl.when(s == S - 1)
-            def _():
-                pltpu.make_async_copy(gtop_ref.at[t], dyn.at[t], topsem.at[t]).wait()
-
+        @pl.when(s == S - 1)
+        def _():
+            pltpu.make_async_copy(gtop_ref.at[t], zin.at[t], topsem.at[t]).wait()
+
+        if not last:
             gr = pl.ds(T * n, n)
 
-            @pl.loop(0, CH + LAG)
-            def _(i):
-                @pl.when((i < CH) & (s > 0))
+            def consume(j, c):
+                cols = arrive(t, c)
+                d = dyn[t, :, cols]
+                lt[2 * t + 3, cols, :] = d.astype(f32).T.astype(bf16)
+                g = jnp.dot(d, wfull[cols, :], preferred_element_type=f32)
+
+                @pl.when(j == 0)
                 def _():
-                    combine(t, i)
-
+                    prod[gr, :] = g
+
+                @pl.when(j > 0)
+                def _():
+                    prod[gr, :] += g
+
+            def service(i):
                 if t == 0:
-                    @pl.when(i == CH // 2)
-                    def _():
-                        l_pass(0)
-
-                    @pl.when(i == CH - 1)
-                    def _():
-                        l_pass(1)
-
-                @pl.when(i >= LAG)
-                def _():
-                    c = i - LAG
-
-                    @pl.when(s < S - 1)
-                    def _():
-                        z_copy(t, c).wait_recv()
-
-                    cols = pl.ds(pl.multiple_of(c * CW, CW), CW)
-                    d = dyn[t, :, cols]
-                    lt[2 * t + 3, cols, :] = d.astype(f32).T.astype(bf16)
-                    g = jnp.dot(d, wfull[cols, :], preferred_element_type=f32)
-
-                    @pl.when(c == 0)
-                    def _():
-                        prod[gr, :] = g
-
-                    @pl.when(c > 0)
-                    def _():
-                        prod[gr, :] += g
-
+                    at_step(i, jnp.where(s == 0, 0, CH - 2), lambda: l_pass(0))
+                    at_step(i, jnp.where(s == 0, CH + LAG - 1, CH), lambda: l_pass(1))
+                    at_step(i, CH + LAG - 1, lambda: r_relay(0))
+
+            relay_loop(t, consume, service)
             l_send(2 * t + 3)
 
             @pl.loop(0, n // rb)
             def _(i):
                 rows = pl.ds(pl.multiple_of(i * rb, rb), rb)
                 g = prod[pl.ds(pl.multiple_of(T * n + i * rb, rb), rb), :]
-                here = pl.ds(pl.multiple_of(mine + i * rb, rb), rb)
-                rhs[2 * t + 2, here, :] = (slope[t + 1, rows, :] * g).astype(bf16)
-        else:
-            for at in range(max(2 * T - 2, 0)):
-                own_rows(at)
-            for part in SPLIT:
+                here_rows = pl.ds(pl.multiple_of(mine + i * rb, rb), rb)
+                rhs[2 * t + 2, here_rows, :] = (slope[t + 1, rows, :] * g).astype(bf16)
+        else:
+            late = len(parts) - 1
+            fill = max(late - 1, 0)
+
+            def consume(j, c):
+                arrive(t, c)
+
+            def begin(at):
+                part = parts[at]
                 l_pass(part)
-
-            @pl.when(s > 0)
-            def _():
-                @pl.loop(0, CH)
-                def _(c):
-                    combine(t, c)
-
-    for at in range(max(2 * T - 2, 0), 2 * T):
-        own_rows(at)
-
-    t = T - 1
-
-    @pl.when(s == S - 1)
-    def _():
-        pltpu.make_async_copy(gtop_ref.at[t], dyn.at[t], topsem.at[t]).wait()
-
-    @pl.when(s < S - 1)
-    def _():
-        @pl.loop(0, CH)
-        def _(c):
-            z_copy(t, c).wait_recv()
-
-    out = pltpu.make_async_copy(dyn.at[t], held_ref.at[0], heldsem.at[0])
-    out.start()
+                r_relay(part)
+                own_wait(part)
+
+            def service(i):
+                if fill > 1:
+                    at_step(i, 0, lambda: r_relay(parts[1]))
+                    at_step(i, jnp.where(s == 0, 0, CH - 2), lambda: l_pass(parts[late]))
+                    at_step(i, CH - 1, lambda: l_pass(parts[fill]))
+                    at_step(i, CH - 1, lambda: r_relay(parts[fill]))
+                for k in range(fill):
+                    @pl.when((i >= k * tiles) & (i < (k + 1) * tiles))
+                    def _():
+                        @pl.when(i == k * tiles)
+                        def _():
+                            begin(k)
+
+                        own_tile(k, i - k * tiles)
+
+            relay_loop(t, consume, service)
+            steps = CH + LAG
+            for k in range(fill):
+                if k * tiles >= steps:
+                    begin(k)
+                for i in range(max(steps - k * tiles, 0), tiles):
+                    own_tile(k, i)
+            if late > 0:
+                begin(fill)
+
+                @pl.loop(0, tiles)
+                def _(i):
+                    own_tile(fill, i)
+
+            begin(late)
 
     for j in range(WCH):
         for k in range(2 * NC - 1):
@@ -427,16 +521,42 @@
         for k in range(2 * NC - 1):
             r_copy(part, k).wait_send()
 
-    @pl.when(s > 0)
-    def _():
-        for t in range(T):
-            @pl.loop(0, CH)
-            def _(c):
+    for t in range(T):
+        @pl.loop(0, CH)
+        def _(c):
+            @pl.when(c < here)
+            def _():
                 for r in range(1, TP):
                     e_copy(t, r, c).wait_send()
-                z_copy(t, c).wait_send()
-
-    out.wait()
+
+            @pl.when(c >= there)
+            def _():
+                for r in range(1, TP):
+                    f_copy(t, r, c).wait_send()
+
+            @pl.when(s > 0)
+            def _():
+                z_copy(t, c, dxs).wait_send()
+
+
+def finish(part, held_in, acc, lta, rhs, held_ref, wg_ref, grad, sem):
+    N = acc.shape[1]
+    nw = pick(N, (256, 128))
+    tiles = N // nw
+    held = pltpu.make_async_copy(held_in, held_ref, sem.at[tiles])
+    held.start()
+
+    def tile_copy(i):
+        cols = pl.ds(i * nw, nw)
+        return pltpu.make_async_copy(grad.at[:, cols], wg_ref.at[0, :, cols], sem.at[i])
+
+    for i in range(tiles):
+        cols = pl.ds(i * nw, nw)
+        grad[:, cols] = acc[:, cols] + jnp.dot(lta[part], rhs[part, :, cols], preferred_element_type=f32)
+        tile_copy(i).start()
+    for i in range(tiles):
+        tile_copy(i).wait()
+    held.wait()
 
 
 def solution(mesh):
@@ -447,25 +567,28 @@
         T = grad_top.shape[0]
         wl, N = weight.shape[1:]
         NC = FS // 2
-        CH = D // pick(D, (384, 256, 128))
-        WCH = 4 if wl % 64 == 0 else 1
+        CH = D // pick(D, (256, 128))
+        WCH = len(w_cuts(wl)) - 1
         K = 2 * NC - 1
         DMA = pltpu.SemaphoreType.DMA
         V = pltpu.VMEM
         any_ = pl.BlockSpec(memory_space=pl.ANY)
+        vmem = pl.BlockSpec(memory_space=V)
         peers = max(TP - 1, 1)
-        held, wg = pl.pallas_call(
+        outs = pl.pallas_call(
             functools.partial(kernel, S, FS, TP, T),
             out_shape=(
-                jax.ShapeDtypeStruct((1, n, D), bf16),
-                jax.ShapeDtypeStruct((1, wl, N), bf16),
+                V((1, n, D), bf16),
+                V((wl, N), f32),
+                V((2 * T, wl, FS * n), bf16),
+                V((2 * T, FS * n, N), bf16),
             ),
             in_specs=[
                 pl.BlockSpec(memory_space=pltpu.SMEM),
                 pl.BlockSpec(memory_space=pltpu.VMEM),
                 any_, any_, any_, any_,
             ],
-            out_specs=(any_, pl.BlockSpec(memory_space=pltpu.VMEM)),
+            out_specs=(vmem,) * 4,
             scratch_shapes=[
                 V((FS * wl, N), bf16),
                 V((MB, n, D), bf16),
@@ -474,27 +597,37 @@
                 V((T, n, 128), f32),
                 V((T, n, D), bf16),
                 V((2 * T, D, n), bf16),
-                V((2 * T, wl, FS * n), bf16),
-                V((2 * T, FS * n, N), bf16),
                 V(((T + 1) * n, N), f32),
                 V((T, n, N), f32),
                 V((T, n, D), bf16),
                 V((T, peers, n, D), bf16),
                 V((T, n, D), bf16),
-                V((wl, N), f32),
-                DMA((3,)), DMA((T,)), DMA((2 * T,)), DMA((1,)),
+                V((T, n, D), bf16),
+                V((T, peers, n, D), bf16),
+                DMA((3,)), DMA((T,)), DMA((2 * T,)),
                 DMA((K, WCH)), DMA((K, WCH)),
                 DMA((2 * T, FS - 1)), DMA((2 * T, FS - 1)),
                 DMA((2 * T, K)), DMA((2 * T, K)),
                 DMA((T, peers, CH)), DMA((T, peers, CH)),
                 DMA((T, CH)), DMA((T, CH)),
                 DMA((2 * T, max(FS - 2, 1), peers)), DMA((2 * T, max(FS - 2, 1), peers)),
+                DMA((T, peers, CH)), DMA((T, peers, CH)),
             ],
             compiler_params=pltpu.CompilerParams(
-                collective_id=0, has_side_effects=True, vmem_limit_bytes=60 * 1024 * 1024
+                collective_id=0, has_side_effects=True, vmem_limit_bytes=44 * 1024 * 1024
             ),
-        )(order, gain, stash, grad_now, grad_top, weight)
-        return held, wg.astype(f32)
+        )(*[pltpu.with_memory_space_constraint(o, pltpu.HBM) for o in (order, gain, stash, grad_now, grad_top, weight)])
+        return pl.pallas_call(
+            functools.partial(finish, 2 * T - 2 if T > 1 else 1),
+            out_shape=(
+                jax.ShapeDtypeStruct((1, n, D), bf16),
+                jax.ShapeDtypeStruct((1, wl, N), f32),
+            ),
+            in_specs=[vmem] * 4,
+            out_specs=(any_, any_),
+            scratch_shapes=[V((wl, N), f32), DMA((N // pick(N, (256, 128)) + 1,))],
+            compiler_params=pltpu.CompilerParams(vmem_limit_bytes=8 * 1024 * 1024),
+        )(*[pltpu.with_memory_space_constraint(o, V) for o in outs])
 
     return jax.shard_map(
         per_device,

time: 85.8 us -> 82.4 us (0.960)
  other arithmetic: 3.02 us -> 0 us
    convert_element_type x1 -> x0, other arithmetic: 3.02 us -> none  [per_device(): return (held, wg.astype(f32))]
    pallas_call x1 -> x2, Pallas kernels: 81.1 us -> 81.6 us  [the longest x1 79.6 us: per_device(): pl.pallas_call(functools.partial(kernel, S, FS, TP, T), out_shape=(V((1,...]
where the time goes in v1:
time: 82.4 us; the launch traced here: 82.2 us
  Pallas kernels  81.6 us (99%)
    pallas_call x1, Pallas kernels, per_device(): pl.pallas_call(functools.partial(kernel, S, FS, TP, T), out_shape=(V((1,...  79.6 us
    pallas_call x1, Pallas kernels, per_device(): pl.pallas_call(functools.partial(finish, 2 * T - 2 if T > 1 else 1), out_...  1.95 us

profile of v1, /device:TPU:0, one launch (start us, length us, event | category | flops | bytes accessed | tf_op | source)
XLA Modules:
  0.0 82.2 jit_solution(4997719419233096154)
XLA Ops:
  0.6 79.6 %shard_map.77 = (bf16[1,128,2304]{2,1,0:T(8,128)(2,1)S(1)}, f32[576,1024]{1,0:T(8,128)S(1)}, bf16[4,576,512]{2,1,0:T(8,128)(2,1)S(1)}, bf16[4,512,1024]{2,1,0:T(8,128)(2,1)S(1)}) custom-call(s32[1,4]{1,0:T(1,128)} %order_ref.1, f32[1,2304]{1,0:T(1,128)} %gain_ref.1, bf16[1,4,128,2304]{3,2,1,0:T(8,128)(2,1)} %stash_ref.1, bf16[1,128,2304]{2,1,0:T(8,128)(2,1)} %gnow_ref.1, ...), custom_call_target="tpu_custom_call" | custom-call | tf_op jit(solution)/shard_map/pallas_call | solution.py:578
  80.3 1.9 %shard_map.78 = (bf16[1,128,2304]{2,1,0:T(8,128)(2,1)}, f32[1,576,1024]{2,1,0:T(8,128)}) custom-call(bf16[1,128,2304]{2,1,0:T(8,128)(2,1)S(1)} %get-tuple-element.6.held_in, f32[576,1024]{1,0:T(8,128)S(1)} %get-tuple-element.7.acc, bf16[4,576,512]{2,1,0:T(8,128)(2,1)S(1)} %get-tuple-element.8.lta, bf16[4,512,1024]{2,1,0:T(8,128)(2,1)S(1)} %get-tuple-element.9.rhs), custom_call_target="tpu_custom_call" | custom-call | tf_op jit(solution)/shard_map/pallas_call | solution.py:620

commit v2 on v1

--- a/solution.py
+++ b/solution.py
@@ -48,13 +48,14 @@
 def kernel(
     S, FS, TP, T, order_ref, gain_ref, stash_ref, gnow_ref, gtop_ref, w_ref,
     held_ref, acc, lta, rhs,
-    wfull, stash, act, xt, inv, dyn, lt, prod, slope, own_e, peer_e, dxs, zin, peer_f,
-    lsem, topsem, ownsem, w_s, w_r, l_s, l_r, r_s, r_r, e_s, e_r, z_s, z_r, x_s, x_r, f_s, f_r,
+    wfull, stash, act, xt, inv, dyn, lt, prod, slope, own_e, peer_e, dxs, zin,
+    lsem, topsem, w_s, w_r, l_s, l_r, r_s, r_r, e_s, e_r, z_s, z_r, x_s, x_r,
 ):
     s = lax.axis_index("section")
     f = lax.axis_index("fsdp")
     p = lax.axis_index("tp")
     NC = FS // 2
+    SPLIT = (0, 1, 2)
     yc = f // 2
     core = f % 2
     sib = 2 * yc + (1 - core)
@@ -69,6 +70,7 @@
     tiles = N // nw
     here = CH * s // S
     there = CH * (s + 1) // S
+    free = jnp.maximum(here, CH - there)
 
     loads = [
         pltpu.make_async_copy(w_ref.at[0], wfull.at[pl.ds(f * wl, wl), :], lsem.at[0]),
@@ -104,21 +106,26 @@
         at = pl.multiple_of(lo + core * (wl - hi - lo), row_step(wl))
         if k < NC:
             rows = pl.ds(pl.multiple_of(f * wl + at, row_step(wl)), hi - lo)
-            src = w_ref.at[0, pl.ds(at, hi - lo), :]
-            to = sib if k == 0 else 2 * ((yc + k) % NC) + core
+            to = 2 * ((yc + k) % NC) + core
         else:
             o = k - NC + 1
             rows = pl.ds(pl.multiple_of((2 * ((yc - o + NC) % NC) + core) * wl + at, row_step(wl)), hi - lo)
-            src = wfull.at[rows, :]
             to = sib
-        return rcopy(src, wfull.at[rows, :], w_s.at[k, j], w_r.at[k, j], {"fsdp": to})
-
-    for k in list(range(1, NC)) + [0]:
+        blk = wfull.at[rows, :]
+        return rcopy(blk, blk, w_s.at[0], w_r.at[1 + (k - 1) * WCH + j], {"fsdp": to})
+
+    def w_sib():
+        blk = wfull.at[pl.ds(pl.multiple_of(f * wl, row_step(wl)), wl), :]
+        return rcopy(blk, blk, w_s.at[0], w_r.at[0], {"fsdp": sib})
+
+    loads[0].wait()
+    for k in range(1, NC):
         for j in range(WCH):
             w_copy(k, j).start()
+    w_sib().start()
 
     def is_split(part):
-        return TP > 1
+        return part in SPLIT and TP > 1
 
     def l_copy(part, k):
         cols = pl.ds(pl.multiple_of(f * n, n), n)
@@ -133,13 +140,13 @@
         else:
             src = lt.at[part, pl.ds(to * wl, wl), :]
             dst = lta.at[part, :, cols]
-        return rcopy(src, dst, l_s.at[part, k], l_r.at[part, k], {"fsdp": to})
+        return rcopy(src, dst, l_s.at[part], l_r.at[part, min(k, 1)], {"fsdp": to})
 
     def x_copy(part, k, q):
         o, cc = (k + 1) // 2, (k - 1) % 2
         src_f = 2 * ((yc - o + NC) % NC) + (core + cc) % 2
         blk = lta.at[part, pl.ds(p * wq, wq), pl.ds(pl.multiple_of(src_f * n, n), n)]
-        return rcopy(blk, blk, x_s.at[part, k - 1, q - 1], x_r.at[part, k - 1, q - 1], {"tp": (p + q) % TP})
+        return rcopy(blk, blk, x_s.at[part], x_r.at[part], {"tp": (p + q) % TP})
 
     passed = set()
 
@@ -147,21 +154,32 @@
         if part in passed or not is_split(part):
             return
         passed.add(part)
+        l_far(part).wait_recv()
         for k in range(1, FS - 1):
-            l_copy(part, k).wait_recv()
             for q in range(1, TP):
                 x_copy(part, k, q).start()
 
-    def l_own(part):
-        return pltpu.make_async_copy(
-            lt.at[part, pl.ds(f * wl, wl), :], lta.at[part, :, pl.ds(pl.multiple_of(f * n, n), n)],
-            ownsem.at[part],
-        )
+    def rows_of(part, rows, ss, rs):
+        blk = lt.at[part, pl.ds(0, rows), :]
+        return rcopy(blk, blk, ss, rs, {"fsdp": sib})
+
+    def l_far(part):
+        return rows_of(part, (FS - 2) * (wq if is_split(part) else wl), l_s.at[part], l_r.at[part, 1])
+
+    def l_sent(part):
+        return rows_of(part, wl + (FS - 2) * (wq if is_split(part) else wl), l_s.at[part], l_r.at[part, 1])
+
+    def x_all(part):
+        return rows_of(part, (FS - 2) * (TP - 1) * wq, x_s.at[part], x_r.at[part])
+
+    def r_rows(part, count, which):
+        blk = rhs.at[part, pl.ds(0, count * n), :]
+        return rcopy(blk, blk, r_s.at[part], r_r.at[part, which], {"fsdp": sib})
 
     def l_send(part):
         for k in list(range(1, FS - 1)) + [0]:
             l_copy(part, k).start()
-        l_own(part).start()
+        lta[part, :, pl.ds(pl.multiple_of(f * n, n), n)] = lt[part, pl.ds(pl.multiple_of(f * wl, row_step(wl)), wl), :]
 
     def r_copy(part, k):
         if k < NC:
@@ -172,7 +190,7 @@
             at = 2 * ((yc - o + NC) % NC) + core
             to = sib
         blk = rhs.at[part, pl.ds(pl.multiple_of(at * n, n), n), :]
-        return rcopy(blk, blk, r_s.at[part, k], r_r.at[part, k], {"fsdp": to})
+        return rcopy(blk, blk, r_s.at[part], r_r.at[part, k if 0 < k < NC else 0], {"fsdp": to})
 
     def r_send(part):
         for k in list(range(1, NC)) + [0]:
@@ -231,9 +249,7 @@
             else:
                 prod[:, cols] += d
 
-    loads[0].wait()
-    for j in range(WCH):
-        w_copy(0, j).wait_recv()
+    w_sib().wait_recv()
     part_product(yc, [(0, half)], True)
     for o in range(1, NC):
         for j in range(WCH):
@@ -269,8 +285,8 @@
     def f_copy(t, r, c):
         cols = pl.ds(pl.multiple_of(c * CW, CW), CW)
         return rcopy(
-            zin.at[t, :, cols], peer_f.at[t, r - 1, :, cols],
-            f_s.at[t, r - 1, c], f_r.at[t, r - 1, c], {"tp": (p + r) % TP},
+            zin.at[t, :, cols], peer_e.at[t, r - 1, :, cols],
+            e_s.at[t, r - 1, c], e_r.at[t, r - 1, c], {"tp": (p + r) % TP},
         )
 
     def z_copy(t, c, src):
@@ -292,7 +308,10 @@
 
         @pl.loop(0, CH)
         def _(i):
-            c = CH - 1 - i
+            both = jnp.minimum(here, CH - here)
+            far_turn = jnp.where(i < 2 * both, i % 2 == 0, CH - here > here)
+            turn = jnp.where(i < 2 * both, i // 2, i - both)
+            c = jnp.where(far_turn, CH - 1 - turn, here - 1 - turn)
             cols = pl.ds(pl.multiple_of(c * CW, CW), CW)
             dh = lax.dot_general(
                 rhs[2 * t, pl.ds(mine, n), :], wfull[cols, :], (((1,), (1,)), ((), ())),
@@ -347,7 +366,7 @@
             total = zin[t, :, cols].astype(f32)
             for r in range(1, TP):
                 f_copy(t, r, c).wait_recv()
-                total = total + peer_f[t, r - 1, :, cols].astype(f32)
+                total = total + peer_e[t, r - 1, :, cols].astype(f32)
             put(t, cols, total.astype(bf16))
 
         return cols
@@ -390,17 +409,12 @@
         parts += [2 * t, 2 * t + 1] if t == 0 else [2 * t + 1, 2 * t]
 
     def own_wait(part):
-        l_own(part).wait()
         l_copy(part, 0).wait_recv()
-        for k in range(1, FS - 1):
-            if is_split(part):
-                for q in range(1, TP):
-                    x_copy(part, k, q).wait_recv()
-            else:
-                l_copy(part, k).wait_recv()
-        r_copy(part, 0).wait_recv()
-        for o in range(1, NC):
-            r_copy(part, NC - 1 + o).wait_recv()
+        if is_split(part):
+            x_all(part).wait_recv()
+        elif FS > 2:
+            l_far(part).wait_recv()
+        r_rows(part, NC, 0).wait_recv()
 
     def own_tile(at, i):
         part = parts[at]
@@ -451,8 +465,7 @@
 
             def service(i):
                 if t == 0:
-                    at_step(i, jnp.where(s == 0, 0, CH - 2), lambda: l_pass(0))
-                    at_step(i, jnp.where(s == 0, CH + LAG - 1, CH), lambda: l_pass(1))
+                    at_step(i, free, lambda: (l_pass(0), l_pass(1)))
                     at_step(i, CH + LAG - 1, lambda: r_relay(0))
 
             relay_loop(t, consume, service)
@@ -480,7 +493,7 @@
             def service(i):
                 if fill > 1:
                     at_step(i, 0, lambda: r_relay(parts[1]))
-                    at_step(i, jnp.where(s == 0, 0, CH - 2), lambda: l_pass(parts[late]))
+                    at_step(i, free, lambda: l_pass(parts[late]))
                     at_step(i, CH - 1, lambda: l_pass(parts[fill]))
                     at_step(i, CH - 1, lambda: r_relay(parts[fill]))
                 for k in range(fill):
@@ -508,31 +521,21 @@
 
             begin(late)
 
-    for j in range(WCH):
-        for k in range(2 * NC - 1):
-            w_copy(k, j).wait_send()
+    w_rows = wfull.at[pl.ds(0, (2 * NC - 1) * wl), :]
+    rcopy(w_rows, w_rows, w_s.at[0], w_r.at[0], {"fsdp": sib}).wait_send()
     for part in range(2 * T):
-        for k in range(FS - 1):
-            l_copy(part, k).wait_send()
-        if is_split(part):
-            for k in range(1, FS - 1):
-                for q in range(1, TP):
-                    x_copy(part, k, q).wait_send()
-        for k in range(2 * NC - 1):
-            r_copy(part, k).wait_send()
+        l_sent(part).wait_send()
+        if is_split(part) and FS > 2:
+            x_all(part).wait_send()
+        r_rows(part, 2 * NC - 1, 0).wait_send()
 
     for t in range(T):
         @pl.loop(0, CH)
         def _(c):
-            @pl.when(c < here)
+            @pl.when((c < here) | (c >= there))
             def _():
                 for r in range(1, TP):
                     e_copy(t, r, c).wait_send()
-
-            @pl.when(c >= there)
-            def _():
-                for r in range(1, TP):
-                    f_copy(t, r, c).wait_send()
 
             @pl.when(s > 0)
             def _():
@@ -603,15 +606,13 @@
                 V((T, peers, n, D), bf16),
                 V((T, n, D), bf16),
                 V((T, n, D), bf16),
-                V((T, peers, n, D), bf16),
-                DMA((3,)), DMA((T,)), DMA((2 * T,)),
-                DMA((K, WCH)), DMA((K, WCH)),
-                DMA((2 * T, FS - 1)), DMA((2 * T, FS - 1)),
-                DMA((2 * T, K)), DMA((2 * T, K)),
+                DMA((3,)), DMA((T,)),
+                DMA((1,)), DMA((1 + (K - 1) * WCH,)),
+                DMA((2 * T,)), DMA((2 * T, 2)),
+                DMA((2 * T,)), DMA((2 * T, NC)),
                 DMA((T, peers, CH)), DMA((T, peers, CH)),
                 DMA((T, CH)), DMA((T, CH)),
-                DMA((2 * T, max(FS - 2, 1), peers)), DMA((2 * T, max(FS - 2, 1), peers)),
-                DMA((T, peers, CH)), DMA((T, peers, CH)),
+                DMA((2 * T,)), DMA((2 * T,)),
             ],
             compiler_params=pltpu.CompilerParams(
                 collective_id=0, has_side_effects=True, vmem_limit_bytes=44 * 1024 * 1024

time: 82.4 us -> 75.2 us (0.913)
  Pallas kernels: 81.6 us -> 74.3 us
    pallas_call x1, Pallas kernels: 79.6 us -> 72.4 us  [per_device(): pl.pallas_call(functools.partial(kernel, S, FS, TP, T), out_shape=(V((1,...]
where the time goes in v2:
time: 75.2 us; the launch traced here: 74.9 us
  Pallas kernels  74.3 us (99%)
    pallas_call x1, Pallas kernels, per_device(): pl.pallas_call(functools.partial(kernel, S, FS, TP, T), out_shape=(V((1,...  72.4 us
    pallas_call x1, Pallas kernels, per_device(): pl.pallas_call(functools.partial(finish, 2 * T - 2 if T > 1 else 1), out_...  1.95 us

profile of v2, /device:TPU:0, one launch (start us, length us, event | category | flops | bytes accessed | tf_op | source)
XLA Modules:
  0.0 74.9 jit_solution(6031770215304069669)
XLA Ops:
  0.6 72.4 %shard_map.77 = (bf16[1,128,2304]{2,1,0:T(8,128)(2,1)S(1)}, f32[576,1024]{1,0:T(8,128)S(1)}, bf16[4,576,512]{2,1,0:T(8,128)(2,1)S(1)}, bf16[4,512,1024]{2,1,0:T(8,128)(2,1)S(1)}) custom-call(s32[1,4]{1,0:T(1,128)} %order_ref.1, f32[1,2304]{1,0:T(1,128)} %gain_ref.1, bf16[1,4,128,2304]{3,2,1,0:T(8,128)(2,1)} %stash_ref.1, bf16[1,128,2304]{2,1,0:T(8,128)(2,1)} %gnow_ref.1, ...), custom_call_target="tpu_custom_call" | custom-call | tf_op jit(solution)/shard_map/pallas_call | solution.py:581
  73.0 1.9 %shard_map.78 = (bf16[1,128,2304]{2,1,0:T(8,128)(2,1)}, f32[1,576,1024]{2,1,0:T(8,128)}) custom-call(bf16[1,128,2304]{2,1,0:T(8,128)(2,1)S(1)} %get-tuple-element.6.held_in, f32[576,1024]{1,0:T(8,128)S(1)} %get-tuple-element.7.acc, bf16[4,576,512]{2,1,0:T(8,128)(2,1)S(1)} %get-tuple-element.8.lta, bf16[4,512,1024]{2,1,0:T(8,128)(2,1)S(1)} %get-tuple-element.9.rhs), custom_call_target="tpu_custom_call" | custom-call | tf_op jit(solution)/shard_map/pallas_call | solution.py:621

commit v3 on v2

--- a/solution.py
+++ b/solution.py
@@ -46,10 +46,10 @@
 
 
 def kernel(
-    S, FS, TP, T, order_ref, gain_ref, stash_ref, gnow_ref, gtop_ref, w_ref,
+    S, FS, TP, T, order_in, gain_in, stash_ref, gnow_ref, gtop_ref, w_ref,
     held_ref, acc, lta, rhs,
-    wfull, stash, act, xt, inv, dyn, lt, prod, slope, own_e, peer_e, dxs, zin,
-    lsem, topsem, w_s, w_r, l_s, l_r, r_s, r_r, e_s, e_r, z_s, z_r, x_s, x_r,
+    order_ref, gain_ref, wfull, stash, act, xt, inv, dyn, lt, prod, slope, own_e, peer_e, dxs, zin,
+    lsem, topsem, w_s, w_r, l_s, l_r, r_s, r_r, e_s, e_r, z_r, x_s, x_r,
 ):
     s = lax.axis_index("section")
     f = lax.axis_index("fsdp")
@@ -76,6 +76,8 @@
         pltpu.make_async_copy(w_ref.at[0], wfull.at[pl.ds(f * wl, wl), :], lsem.at[0]),
         pltpu.make_async_copy(stash_ref.at[0], stash, lsem.at[1]),
         pltpu.make_async_copy(gnow_ref.at[0], act.at[pl.ds(T * n, n), :], lsem.at[2]),
+        pltpu.make_async_copy(order_in, order_ref, lsem.at[3]),
+        pltpu.make_async_copy(gain_in, gain_ref, lsem.at[4]),
     ]
     for c in loads:
         c.start()
@@ -154,6 +156,9 @@
         if part in passed or not is_split(part):
             return
         passed.add(part)
+        l_forward(part)
+
+    def l_forward(part):
         l_far(part).wait_recv()
         for k in range(1, FS - 1):
             for q in range(1, TP):
@@ -204,6 +209,8 @@
             cols = pl.ds(pl.multiple_of(i * tw, tw), tw)
             lt[part, cols, :] = ref[pl.ds(first, n), cols].astype(f32).T.astype(bf16)
 
+    loads[3].wait()
+    loads[4].wait()
     loads[1].wait()
     rb = pick(n, (32, 16))
     for t in range(T):
@@ -279,21 +286,21 @@
         cols = pl.ds(pl.multiple_of(c * CW, CW), CW)
         return rcopy(
             own_e.at[t, :, cols], peer_e.at[t, r - 1, :, cols],
-            e_s.at[t, r - 1, c], e_r.at[t, r - 1, c], {"tp": (p + r) % TP},
+            e_s.at[t, c], e_r.at[t, r - 1, c], {"tp": (p + r) % TP},
         )
 
     def f_copy(t, r, c):
         cols = pl.ds(pl.multiple_of(c * CW, CW), CW)
         return rcopy(
             zin.at[t, :, cols], peer_e.at[t, r - 1, :, cols],
-            e_s.at[t, r - 1, c], e_r.at[t, r - 1, c], {"tp": (p + r) % TP},
+            e_s.at[t, c], e_r.at[t, r - 1, c], {"tp": (p + r) % TP},
         )
 
     def z_copy(t, c, src):
         cols = pl.ds(pl.multiple_of(c * CW, CW), CW)
         to = jnp.maximum(s - 1, 0)
         return rcopy(
-            src.at[t, :, cols], zin.at[t, :, cols], z_s.at[t, c], z_r.at[t, c], {"section": to}
+            src.at[t, :, cols], zin.at[t, :, cols], e_s.at[t, c], z_r.at[t, c], {"section": to}
         )
 
     def held_dy(t, cols):
@@ -406,7 +413,7 @@
 
     parts = []
     for t in range(T):
-        parts += [2 * t, 2 * t + 1] if t == 0 else [2 * t + 1, 2 * t]
+        parts += [2 * t, 2 * t + 1]
 
     def own_wait(part):
         l_copy(part, 0).wait_recv()
@@ -424,6 +431,35 @@
             d = acc[:, cols] + d
         acc[:, cols] = d
 
+    def sent():
+        w_rows = wfull.at[pl.ds(0, (2 * NC - 1) * wl), :]
+        rcopy(w_rows, w_rows, w_s.at[0], w_r.at[0], {"fsdp": sib}).wait_send()
+        for part in range(2 * T):
+            l_sent(part).wait_send()
+            if is_split(part) and FS > 2:
+                x_all(part).wait_send()
+        for t in range(T):
+            @pl.loop(0, CH)
+            def _(c):
+                crossed = (c < here) | (c >= there)
+
+                @pl.when(crossed & (s > 0))
+                def _():
+                    chunk_sent(t, c, TP)
+
+                @pl.when(crossed & (s == 0))
+                def _():
+                    chunk_sent(t, c, TP - 1)
+
+                @pl.when(jnp.logical_not(crossed) & (s > 0))
+                def _():
+                    chunk_sent(t, c, 1)
+
+    def chunk_sent(t, c, count):
+        blk = own_e.at[t, :, pl.ds(0, count * CW)]
+        if count > 0:
+            rcopy(blk, blk, e_s.at[t, c], z_r.at[t, c], {"fsdp": sib}).wait_send()
+
     for t in range(T):
         last = t == T - 1
         if t == 0:
@@ -432,6 +468,7 @@
             r_send(1)
         else:
             r_send(2 * t)
+            l_send(2 * t + 1)
 
         @pl.when(s > 0)
         def _():
@@ -465,11 +502,20 @@
 
             def service(i):
                 if t == 0:
-                    at_step(i, free, lambda: (l_pass(0), l_pass(1)))
+                    if is_split(0):
+                        passed.add(0)
+                        at_step(i, jnp.where(s == 0, -1, free), lambda: l_forward(0))
+                    at_step(i, free, lambda: l_pass(1))
                     at_step(i, CH + LAG - 1, lambda: r_relay(0))
+                    if is_split(2):
+                        at_step(i, jnp.where(s == 0, CH + LAG - 1, -1), lambda: l_forward(2))
+
+            if t == 0 and is_split(0):
+                @pl.when(s == 0)
+                def _():
+                    l_forward(0)
 
             relay_loop(t, consume, service)
-            l_send(2 * t + 3)
 
             @pl.loop(0, n // rb)
             def _(i):
@@ -479,7 +525,7 @@
                 rhs[2 * t + 2, here_rows, :] = (slope[t + 1, rows, :] * g).astype(bf16)
         else:
             late = len(parts) - 1
-            fill = max(late - 1, 0)
+            steps = CH + LAG
 
             def consume(j, c):
                 arrive(t, c)
@@ -491,55 +537,35 @@
                 own_wait(part)
 
             def service(i):
-                if fill > 1:
+                if late > 2:
                     at_step(i, 0, lambda: r_relay(parts[1]))
-                    at_step(i, free, lambda: l_pass(parts[late]))
-                    at_step(i, CH - 1, lambda: l_pass(parts[fill]))
-                    at_step(i, CH - 1, lambda: r_relay(parts[fill]))
-                for k in range(fill):
-                    @pl.when((i >= k * tiles) & (i < (k + 1) * tiles))
+                    if is_split(2):
+                        passed.add(2)
+                        at_step(i, jnp.where(s == 0, -1, free), lambda: l_forward(2))
+                    at_step(i, CH - 1, lambda: (r_relay(parts[late]), r_relay(parts[2])))
+                for k in range(late):
+                    first = k * tiles + (k > 1)
+
+                    @pl.when((i >= first) & (i < first + tiles))
                     def _():
-                        @pl.when(i == k * tiles)
+                        @pl.when(i == first)
                         def _():
                             begin(k)
 
-                        own_tile(k, i - k * tiles)
+                        own_tile(k, i - first)
 
             relay_loop(t, consume, service)
-            steps = CH + LAG
-            for k in range(fill):
-                if k * tiles >= steps:
+            for k in range(late):
+                first = k * tiles + (k > 1)
+                if first >= steps:
                     begin(k)
-                for i in range(max(steps - k * tiles, 0), tiles):
+                for i in range(max(steps - first, 0), tiles):
                     own_tile(k, i)
-            if late > 0:
-                begin(fill)
-
-                @pl.loop(0, tiles)
-                def _(i):
-                    own_tile(fill, i)
-
+            sent()
             begin(late)
 
-    w_rows = wfull.at[pl.ds(0, (2 * NC - 1) * wl), :]
-    rcopy(w_rows, w_rows, w_s.at[0], w_r.at[0], {"fsdp": sib}).wait_send()
     for part in range(2 * T):
-        l_sent(part).wait_send()
-        if is_split(part) and FS > 2:
-            x_all(part).wait_send()
         r_rows(part, 2 * NC - 1, 0).wait_send()
-
-    for t in range(T):
-        @pl.loop(0, CH)
-        def _(c):
-            @pl.when((c < here) | (c >= there))
-            def _():
-                for r in range(1, TP):
-                    e_copy(t, r, c).wait_send()
-
-            @pl.when(s > 0)
-            def _():
-                z_copy(t, c, dxs).wait_send()
 
 
 def finish(part, held_in, acc, lta, rhs, held_ref, wg_ref, grad, sem):
@@ -587,12 +613,12 @@
                 V((2 * T, FS * n, N), bf16),
             ),
             in_specs=[
-                pl.BlockSpec(memory_space=pltpu.SMEM),
-                pl.BlockSpec(memory_space=pltpu.VMEM),
-                any_, any_, any_, any_,
+                any_, any_, any_, any_, any_, any_,
             ],
             out_specs=(vmem,) * 4,
             scratch_shapes=[
+                pltpu.SMEM((1, MB), jnp.int32),
+                V((1, D), f32),
                 V((FS * wl, N), bf16),
                 V((MB, n, D), bf16),
                 V(((T + 1) * n, D), bf16),
@@ -606,12 +632,11 @@
                 V((T, peers, n, D), bf16),
                 V((T, n, D), bf16),
                 V((T, n, D), bf16),
-                DMA((3,)), DMA((T,)),
+                DMA((5,)), DMA((T,)),
                 DMA((1,)), DMA((1 + (K - 1) * WCH,)),
                 DMA((2 * T,)), DMA((2 * T, 2)),
                 DMA((2 * T,)), DMA((2 * T, NC)),
-                DMA((T, peers, CH)), DMA((T, peers, CH)),
-                DMA((T, CH)), DMA((T, CH)),
+                DMA((T, CH)), DMA((T, peers, CH)), DMA((T, CH)),
                 DMA((2 * T,)), DMA((2 * T,)),
             ],
             compiler_params=pltpu.CompilerParams(
@@ -619,7 +644,7 @@
             ),
         )(*[pltpu.with_memory_space_constraint(o, pltpu.HBM) for o in (order, gain, stash, grad_now, grad_top, weight)])
         return pl.pallas_call(
-            functools.partial(finish, 2 * T - 2 if T > 1 else 1),
+            functools.partial(finish, 2 * T - 1),
             out_shape=(
                 jax.ShapeDtypeStruct((1, n, D), bf16),
                 jax.ShapeDtypeStruct((1, wl, N), f32),

time: 75.2 us -> 72.2 us (0.960)
  Pallas kernels: 74.3 us -> 71.4 us
    pallas_call x1, Pallas kernels: 72.4 us -> 69.5 us  [per_device(): pl.pallas_call(functools.partial(kernel, S, FS, TP, T), out_shape=(V((1,...]
where the time goes in v3:
time: 72.2 us; the launch traced here: 72.1 us
  Pallas kernels  71.4 us (99%)
    pallas_call x1, Pallas kernels, per_device(): pl.pallas_call(functools.partial(kernel, S, FS, TP, T), out_shape=(V((1,...  69.5 us
    pallas_call x1, Pallas kernels, per_device(): pl.pallas_call(functools.partial(finish, 2 * T - 1), out_shape=(jax.Shape...  1.95 us

profile of v3, /device:TPU:0, one launch (start us, length us, event | category | flops | bytes accessed | tf_op | source)
XLA Modules:
  0.0 72.1 jit_solution(5111189071725350917)
XLA Ops:
  0.6 69.5 %shard_map.77 = (bf16[1,128,2304]{2,1,0:T(8,128)(2,1)S(1)}, f32[576,1024]{1,0:T(8,128)S(1)}, bf16[4,576,512]{2,1,0:T(8,128)(2,1)S(1)}, bf16[4,512,1024]{2,1,0:T(8,128)(2,1)S(1)}) custom-call(s32[1,4]{1,0:T(1,128)} %order_in.1, f32[1,2304]{1,0:T(1,128)} %gain_in.1, bf16[1,4,128,2304]{3,2,1,0:T(8,128)(2,1)} %stash_ref.1, bf16[1,128,2304]{2,1,0:T(8,128)(2,1)} %gnow_ref.1, ...), custom_call_target="tpu_custom_call" | custom-call | tf_op jit(solution)/shard_map/pallas_call | solution.py:607
  70.1 2.0 %shard_map.78 = (bf16[1,128,2304]{2,1,0:T(8,128)(2,1)}, f32[1,576,1024]{2,1,0:T(8,128)}) custom-call(bf16[1,128,2304]{2,1,0:T(8,128)(2,1)S(1)} %get-tuple-element.6.held_in, f32[576,1024]{1,0:T(8,128)S(1)} %get-tuple-element.7.acc, bf16[4,576,512]{2,1,0:T(8,128)(2,1)S(1)} %get-tuple-element.8.lta, bf16[4,512,1024]{2,1,0:T(8,128)(2,1)S(1)} %get-tuple-element.9.rhs), custom_call_target="tpu_custom_call" | custom-call | tf_op jit(solution)/shard_map/pallas_call | solution.py:646

commit v4 on v3

--- a/solution.py
+++ b/solution.py
@@ -242,10 +242,10 @@
 
     half = 2 * wl
 
-    def part_product(chip, spans, first):
-        @pl.loop(0, tiles)
+    def part_product(chip, spans, first, width):
+        @pl.loop(0, N // width)
         def _(i):
-            cols = pl.ds(pl.multiple_of(i * nw, nw), nw)
+            cols = pl.ds(pl.multiple_of(i * width, width), width)
             d = None
             for lo, hi in spans:
                 ks = pl.ds(pl.multiple_of(chip * half + lo, math.gcd(half, lo)), hi - lo)
@@ -257,7 +257,7 @@
                 prod[:, cols] += d
 
     w_sib().wait_recv()
-    part_product(yc, [(0, half)], True)
+    part_product(yc, [(0, half)], True, nw)
     for o in range(1, NC):
         for j in range(WCH):
             w_copy(o, j).wait_recv()
@@ -265,7 +265,7 @@
             w_copy(NC - 1 + o, j).wait_recv()
             lo, hi = cuts[j], cuts[j + 1]
             spans = [(lo, half - lo)] if hi == wl else [(lo, hi), (half - hi, half - lo)]
-            part_product((yc - o + NC) % NC, spans, False)
+            part_product((yc - o + NC) % NC, spans, False, N if hi == wl and 0 < lo else nw)
 
     mine = pl.multiple_of(f * n, n)
 

time: 72.2 us -> 71.8 us (level)
  no operation moved by 1% of the time
where the time goes in v4:
time: 71.8 us; the launch traced here: 71.6 us
  Pallas kernels  71 us (99%)
    pallas_call x1, Pallas kernels, per_device(): pl.pallas_call(functools.partial(kernel, S, FS, TP, T), out_shape=(V((1,...  69 us
    pallas_call x1, Pallas kernels, per_device(): pl.pallas_call(functools.partial(finish, 2 * T - 1), out_shape=(jax.Shape...  1.95 us

profile of v4, /device:TPU:0, one launch (start us, length us, event | category | flops | bytes accessed | tf_op | source)
XLA Modules:
  0.0 71.6 jit_solution(2387673289803593589)
XLA Ops:
  0.6 69.0 %shard_map.77 = (bf16[1,128,2304]{2,1,0:T(8,128)(2,1)S(1)}, f32[576,1024]{1,0:T(8,128)S(1)}, bf16[4,576,512]{2,1,0:T(8,128)(2,1)S(1)}, bf16[4,512,1024]{2,1,0:T(8,128)(2,1)S(1)}) custom-call(s32[1,4]{1,0:T(1,128)} %order_in.1, f32[1,2304]{1,0:T(1,128)} %gain_in.1, bf16[1,4,128,2304]{3,2,1,0:T(8,128)(2,1)} %stash_ref.1, bf16[1,128,2304]{2,1,0:T(8,128)(2,1)} %gnow_ref.1, ...), custom_call_target="tpu_custom_call" | custom-call | tf_op jit(solution)/shard_map/pallas_call | solution.py:607
  69.6 2.0 %shard_map.78 = (bf16[1,128,2304]{2,1,0:T(8,128)(2,1)}, f32[1,576,1024]{2,1,0:T(8,128)}) custom-call(bf16[1,128,2304]{2,1,0:T(8,128)(2,1)S(1)} %get-tuple-element.6.held_in, f32[576,1024]{1,0:T(8,128)S(1)} %get-tuple-element.7.acc, bf16[4,576,512]{2,1,0:T(8,128)(2,1)S(1)} %get-tuple-element.8.lta, bf16[4,512,1024]{2,1,0:T(8,128)(2,1)S(1)} %get-tuple-element.9.rhs), custom_call_target="tpu_custom_call" | custom-call | tf_op jit(solution)/shard_map/pallas_call | solution.py:646

commit v5 on v4

--- a/solution.py
+++ b/solution.py
@@ -12,7 +12,7 @@
 MESH = pl.DeviceIdType.MESH
 f32 = jnp.float32
 bf16 = jnp.bfloat16
-LAG = 3
+LAG = 4
 
 
 def gelu_parts(u):
@@ -569,19 +569,19 @@
 
 
 def finish(part, held_in, acc, lta, rhs, held_ref, wg_ref, grad, sem):
-    N = acc.shape[1]
-    nw = pick(N, (256, 128))
-    tiles = N // nw
+    wl = acc.shape[0]
+    tiles = 4
+    step = wl // tiles
     held = pltpu.make_async_copy(held_in, held_ref, sem.at[tiles])
     held.start()
 
     def tile_copy(i):
-        cols = pl.ds(i * nw, nw)
-        return pltpu.make_async_copy(grad.at[:, cols], wg_ref.at[0, :, cols], sem.at[i])
+        rows = pl.ds(i * step, step)
+        return pltpu.make_async_copy(grad.at[rows, :], wg_ref.at[0, rows, :], sem.at[i])
 
     for i in range(tiles):
-        cols = pl.ds(i * nw, nw)
-        grad[:, cols] = acc[:, cols] + jnp.dot(lta[part], rhs[part, :, cols], preferred_element_type=f32)
+        rows = pl.ds(i * step, step)
+        grad[rows, :] = acc[rows, :] + jnp.dot(lta[part, rows, :], rhs[part], preferred_element_type=f32)
         tile_copy(i).start()
     for i in range(tiles):
         tile_copy(i).wait()
@@ -651,7 +651,7 @@
             ),
             in_specs=[vmem] * 4,
             out_specs=(any_, any_),
-            scratch_shapes=[V((wl, N), f32), DMA((N // pick(N, (256, 128)) + 1,))],
+            scratch_shapes=[V((wl, N), f32), DMA((9,))],
             compiler_params=pltpu.CompilerParams(vmem_limit_bytes=8 * 1024 * 1024),
         )(*[pltpu.with_memory_space_constraint(o, V) for o in outs])
 

time: 71.8 us -> 71.5 us (level)
  no operation moved by 1% of the time
where the time goes in v5:
time: 71.5 us; the launch traced here: 71.2 us
  Pallas kernels  70.5 us (99%)
    pallas_call x1, Pallas kernels, per_device(): pl.pallas_call(functools.partial(kernel, S, FS, TP, T), out_shape=(V((1,...  68.7 us
    pallas_call x1, Pallas kernels, per_device(): pl.pallas_call(functools.partial(finish, 2 * T - 1), out_shape=(jax.Shape...  1.82 us

profile of v5, /device:TPU:0, one launch (start us, length us, event | category | flops | bytes accessed | tf_op | source)
XLA Modules:
  0.0 71.2 jit_solution(2752863131414427779)
XLA Ops:
  0.6 68.7 %shard_map.77 = (bf16[1,128,2304]{2,1,0:T(8,128)(2,1)S(1)}, f32[576,1024]{1,0:T(8,128)S(1)}, bf16[4,576,512]{2,1,0:T(8,128)(2,1)S(1)}, bf16[4,512,1024]{2,1,0:T(8,128)(2,1)S(1)}) custom-call(s32[1,4]{1,0:T(1,128)} %order_in.1, f32[1,2304]{1,0:T(1,128)} %gain_in.1, bf16[1,4,128,2304]{3,2,1,0:T(8,128)(2,1)} %stash_ref.1, bf16[1,128,2304]{2,1,0:T(8,128)(2,1)} %gnow_ref.1, ...), custom_call_target="tpu_custom_call" | custom-call | tf_op jit(solution)/shard_map/pallas_call | solution.py:607
  69.3 1.8 %shard_map.78 = (bf16[1,128,2304]{2,1,0:T(8,128)(2,1)}, f32[1,576,1024]{2,1,0:T(8,128)}) custom-call(bf16[1,128,2304]{2,1,0:T(8,128)(2,1)S(1)} %get-tuple-element.6.held_in, f32[576,1024]{1,0:T(8,128)S(1)} %get-tuple-element.7.acc, bf16[4,576,512]{2,1,0:T(8,128)(2,1)S(1)} %get-tuple-element.8.lta, bf16[4,512,1024]{2,1,0:T(8,128)(2,1)S(1)} %get-tuple-element.9.rhs), custom_call_target="tpu_custom_call" | custom-call | tf_op jit(solution)/shard_map/pallas_call | solution.py:646

commit v6 on v5

--- a/solution.py
+++ b/solution.py
@@ -79,9 +79,6 @@
         pltpu.make_async_copy(order_in, order_ref, lsem.at[3]),
         pltpu.make_async_copy(gain_in, gain_ref, lsem.at[4]),
     ]
-    for c in loads:
-        c.start()
-
     bar = pltpu.get_barrier_semaphore()
     for r in range(1, FS):
         pl.semaphore_signal(bar, inc=1, device_id={"fsdp": (f + r) % FS}, device_id_type=MESH)
@@ -95,6 +92,9 @@
     @pl.when(s < S - 1)
     def _():
         pl.semaphore_signal(bar, inc=1, device_id={"section": s + 1}, device_id_type=MESH)
+
+    for c in loads:
+        c.start()
 
     pl.semaphore_wait(bar, FS - 1 + TP - 1 + jnp.minimum(s, 1) + jnp.minimum(S - 1 - s, 1))
 
@@ -195,7 +195,7 @@
             at = 2 * ((yc - o + NC) % NC) + core
             to = sib
         blk = rhs.at[part, pl.ds(pl.multiple_of(at * n, n), n), :]
-        return rcopy(blk, blk, r_s.at[part], r_r.at[part, k if 0 < k < NC else 0], {"fsdp": to})
+        return rcopy(blk, blk, r_s.at[part], r_r.at[part, min(k, NC)], {"fsdp": to})
 
     def r_send(part):
         for k in list(range(1, NC)) + [0]:
@@ -416,12 +416,29 @@
         parts += [2 * t, 2 * t + 1]
 
     def own_wait(part):
+        chip_wait(part)
+        far_wait(part)
+
+    def chip_wait(part):
         l_copy(part, 0).wait_recv()
+        r_copy(part, 0).wait_recv()
+
+    def far_wait(part):
         if is_split(part):
             x_all(part).wait_recv()
         elif FS > 2:
             l_far(part).wait_recv()
-        r_rows(part, NC, 0).wait_recv()
+        if NC > 1:
+            r_rows(part, NC - 1, NC).wait_recv()
+
+    def chip_tile(at, i, chips):
+        part = parts[at]
+        cols = pl.ds(pl.multiple_of(i * nw, nw), nw)
+        d = acc[:, cols]
+        for o in chips:
+            ks = pl.ds(pl.multiple_of((yc + o) % NC * (2 * n), 2 * n), 2 * n)
+            d = d + jnp.dot(lta[part, :, ks], rhs[part, ks, cols], preferred_element_type=f32)
+        acc[:, cols] = d
 
     def own_tile(at, i):
         part = parts[at]
@@ -526,6 +543,9 @@
         else:
             late = len(parts) - 1
             steps = CH + LAG
+            near_at, far_at = tiles, steps - tiles
+            halves = late > 1 and NC > 1 and 2 * tiles <= far_at
+            whole = late - 1 if halves else late
 
             def consume(j, c):
                 arrive(t, c)
@@ -543,23 +563,41 @@
                         passed.add(2)
                         at_step(i, jnp.where(s == 0, -1, free), lambda: l_forward(2))
                     at_step(i, CH - 1, lambda: (r_relay(parts[late]), r_relay(parts[2])))
-                for k in range(late):
-                    first = k * tiles + (k > 1)
-
-                    @pl.when((i >= first) & (i < first + tiles))
+                for k in range(whole):
+                    @pl.when((i >= k * tiles) & (i < (k + 1) * tiles))
                     def _():
-                        @pl.when(i == first)
+                        @pl.when(i == k * tiles)
                         def _():
                             begin(k)
 
-                        own_tile(k, i - first)
+                        own_tile(k, i - k * tiles)
+
+                if halves:
+                    k = late - 1
+
+                    @pl.when((i >= near_at) & (i < near_at + tiles))
+                    def _():
+                        @pl.when(i == near_at)
+                        def _():
+                            chip_wait(parts[k])
+
+                        chip_tile(k, i - near_at, [0])
+
+                    @pl.when((i >= far_at) & (i < far_at + tiles))
+                    def _():
+                        @pl.when(i == far_at)
+                        def _():
+                            l_pass(parts[k])
+                            r_relay(parts[k])
+                            far_wait(parts[k])
+
+                        chip_tile(k, i - far_at, range(1, NC))
 
             relay_loop(t, consume, service)
-            for k in range(late):
-                first = k * tiles + (k > 1)
-                if first >= steps:
+            for k in range(whole):
+                if k * tiles >= steps:
                     begin(k)
-                for i in range(max(steps - first, 0), tiles):
+                for i in range(max(steps - k * tiles, 0), tiles):
                     own_tile(k, i)
             sent()
             begin(late)
@@ -635,7 +673,7 @@
                 DMA((5,)), DMA((T,)),
                 DMA((1,)), DMA((1 + (K - 1) * WCH,)),
                 DMA((2 * T,)), DMA((2 * T, 2)),
-                DMA((2 * T,)), DMA((2 * T, NC)),
+                DMA((2 * T,)), DMA((2 * T, NC + 1)),
                 DMA((T, CH)), DMA((T, peers, CH)), DMA((T, CH)),
                 DMA((2 * T,)), DMA((2 * T,)),
             ],

time: 71.5 us -> 71.5 us (level)
  no operation moved by 1% of the time
where the time goes in v6:
time: 71.5 us; the launch traced here: 71 us
  Pallas kernels  70.4 us (98%)
    pallas_call x1, Pallas kernels, per_device(): pl.pallas_call(functools.partial(kernel, S, FS, TP, T), out_shape=(V((1,...  68.6 us
    pallas_call x1, Pallas kernels, per_device(): pl.pallas_call(functools.partial(finish, 2 * T - 1), out_shape=(jax.Shape...  1.81 us

profile of v6, /device:TPU:0, one launch (start us, length us, event | category | flops | bytes accessed | tf_op | source)
XLA Modules:
  0.0 71.0 jit_solution(15328377657774054321)
XLA Ops:
  0.6 68.6 %shard_map.77 = (bf16[1,128,2304]{2,1,0:T(8,128)(2,1)S(1)}, f32[576,1024]{1,0:T(8,128)S(1)}, bf16[4,576,512]{2,1,0:T(8,128)(2,1)S(1)}, bf16[4,512,1024]{2,1,0:T(8,128)(2,1)S(1)}) custom-call(s32[1,4]{1,0:T(1,128)} %order_in.1, f32[1,2304]{1,0:T(1,128)} %gain_in.1, bf16[1,4,128,2304]{3,2,1,0:T(8,128)(2,1)} %stash_ref.1, bf16[1,128,2304]{2,1,0:T(8,128)(2,1)} %gnow_ref.1, ...), custom_call_target="tpu_custom_call" | custom-call | tf_op jit(solution)/shard_map/pallas_call | solution.py:645
  69.2 1.8 %shard_map.78 = (bf16[1,128,2304]{2,1,0:T(8,128)(2,1)}, f32[1,576,1024]{2,1,0:T(8,128)}) custom-call(bf16[1,128,2304]{2,1,0:T(8,128)(2,1)S(1)} %get-tuple-element.6.held_in, f32[576,1024]{1,0:T(8,128)S(1)} %get-tuple-element.7.acc, bf16[4,576,512]{2,1,0:T(8,128)(2,1)S(1)} %get-tuple-element.8.lta, bf16[4,512,1024]{2,1,0:T(8,128)(2,1)S(1)} %get-tuple-element.9.rhs), custom_call_target="tpu_custom_call" | custom-call | tf_op jit(solution)/shard_map/pallas_call | solution.py:684
